TPU v7x, 32 devices: a whole 2x2x4 slice. The times are simulated.
32 devices in a mesh: section: 4 (over y, core), sim: 8 (over z, x).
Axes of the slice: x: 2, y: 2, z: 4, core: 2. Of those that a mesh axis runs over, the one named last changes fastest.
Arguments:
- state: float32 [128, 64, 8192], P('section', None, 'sim'), may hold values from -60 to 60
- owner: int32 [128, 1], P('section'), may hold values from 0 to 7; in each aligned block of 32 rows (0 to 31, 32 to 63, ...) at most 8 rows name the same one
- counts: int32 [128], P('section'), may hold values from 2048 to 8192
Outputs:
- slab_mean: float32 [128, 64], P('section')
- slab_cov: float32 [128, 4096], P('section', 'sim')
- group_cov: float32 [32, 4096], P(('section', 'sim'))
- global_mean: float32 [64], replicated
- global_cov: float32 [64, 64], replicated
Inputs may be any that keep to these rules, and one draw needn't show every extreme that they name: Among the 32 slabs of one group, no owner is named by more than 8 slabs, and one owner is named by exactly 8 slabs in some or all groups.
All inputs are finite; a program needn't handle non-finite values.
Results may differ from a plain program's by a relative error of at most 0.0003.
Values sent between devices are 32-bit elements; how exact they have to be, the bound alone decides.
A program may use at most 64 MiB of HBM per device.

v0:
```python
import jax
import jax.numpy as jnp
from jax import lax
from jax.sharding import PartitionSpec as P


def slot_payload(number, mean, comoment, capacity, n_sim, width):
    slot_cov = comoment / jnp.maximum(number - 1.0, 1.0)[:, None]
    cov_parts = slot_cov.reshape(capacity, n_sim, width * width // n_sim)
    mean_copies = jnp.broadcast_to(mean[:, None, :], (capacity, n_sim, width))
    return (cov_parts, mean_copies)


def owner_stats(number, mean, comoment):
    high = lax.Precision.HIGHEST
    width = mean.shape[1]
    group_count = jnp.sum(number)
    group_mean = jnp.sum(number[:, None] * mean, axis=0) / jnp.maximum(group_count, 1.0)
    offset = mean - group_mean[None, :]
    group_co = jnp.sum(comoment, axis=0) + jnp.einsum(
        "k,kv,kw->vw", number, offset, offset, precision=high
    ).reshape(width * width)
    return (group_count, group_mean, group_co)


def local(state, owner, counts):
    high = lax.Precision.HIGHEST
    slab_here, width, cells_dev = state.shape
    n_sim = lax.axis_size("sim")
    my_index = lax.axis_index("sim")
    capacity = 2 * slab_here // n_sim
    slots = n_sim * capacity
    target = owner[:, 0]
    order = jnp.arange(slab_here, dtype=jnp.int32)
    earlier = (target[:, None] == target[None, :]) & (order[None, :] < order[:, None])
    rank = jnp.sum(earlier.astype(jnp.int32), axis=1)
    slot_of = target * capacity + rank
    match = slot_of[:, None] == jnp.arange(slots, dtype=jnp.int32)[None, :]
    filled = jnp.any(match, axis=0)
    source_slab = jnp.sum(jnp.where(match, order[:, None], 0), axis=0)
    tile_start = my_index * cells_dev
    tile_count = jnp.clip(counts - tile_start, 0, cells_dev).astype(jnp.float32)
    live = jnp.arange(cells_dev, dtype=jnp.int32)[None, :] + tile_start < counts[:, None]
    tile_mean = (
        jnp.sum(jnp.where(live[:, None, :], state, 0.0), axis=2)
        / jnp.maximum(tile_count, 1.0)[:, None]
    )
    centered = jnp.where(live[:, None, :], state - tile_mean[:, :, None], 0.0)
    tile_co = jnp.einsum("svc,swc->svw", centered, centered, precision=high).reshape(
        slab_here, width * width
    )
    send_mean = jnp.where(filled[:, None], tile_mean[source_slab], 0.0).reshape(
        n_sim, capacity, width
    )
    send_co = jnp.where(filled[:, None], tile_co[source_slab], 0.0).reshape(
        n_sim, capacity, width * width
    )
    send_count = jnp.where(filled, tile_count[source_slab], 0.0).reshape(n_sim, capacity)
    means = lax.all_to_all(send_mean, "sim", split_axis=0, concat_axis=0, tiled=True)
    comoms = lax.all_to_all(send_co, "sim", split_axis=0, concat_axis=0, tiled=True)
    amounts = lax.all_to_all(send_count, "sim", split_axis=0, concat_axis=0, tiled=True)
    number = jnp.sum(amounts, axis=0)
    mean = jnp.sum(amounts[:, :, None] * means, axis=0) / jnp.maximum(number, 1.0)[:, None]
    offset = means - mean[None, :, :]
    extra = jnp.einsum("ik,ikv,ikw->kvw", amounts, offset, offset, precision=high)
    number, mean, comoment = (
        number,
        mean,
        jnp.sum(comoms, axis=0) + extra.reshape(number.shape[0], width * width),
    )
    cov_parts, mean_copies = slot_payload(number, mean, comoment, capacity, n_sim, width)
    back_cov, back_mean = (
        lax.all_to_all(cov_parts, "sim", split_axis=1, concat_axis=0, tiled=True),
        lax.all_to_all(mean_copies, "sim", split_axis=1, concat_axis=0, tiled=True),
    )
    slab_cov = back_cov[slot_of, 0]
    slab_mean = back_mean[slot_of, 0]
    group_count, group_mean, group_co = owner_stats(number, mean, comoment)
    group_cov = (group_co / jnp.maximum(group_count - 1.0, 1.0))[None, :]
    total, weighted = lax.psum((group_count, group_count * group_mean), ("section", "sim"))
    global_mean = weighted / total
    gap = group_mean - global_mean
    spread = lax.psum(group_co + group_count * jnp.outer(gap, gap).reshape(-1), ("section", "sim"))
    global_cov = (spread / (total - 1.0)).reshape(width, width)
    return (slab_mean, slab_cov, group_cov, global_mean, global_cov)


def solution(mesh):
    return jax.shard_map(
        local,
        mesh=mesh,
        in_specs=(P("section", None, "sim"), P("section", None), P("section")),
        out_specs=(P("section", None), P("section", "sim"), P(("section", "sim"), None), P(), P()),
        check_vma=False,
    )
```

profile of v0, /device:TPU:0, one launch (start us, length us, event | category | flops | bytes accessed | tf_op | source)
XLA Modules:
  0.0 160.8 jit_solution(15916009984353185825)
XLA Ops:
  0.6 0.9 convert_reduce_fusion
  1.5 0.7 fusion.19
  2.2 0.1 fusion.10
  2.3 0.1 select_reduce_fusion.1
  2.4 0.7 broadcast_maximum_fusion.1
  3.1 0.8 gather_fusion
  3.9 0.7 select_n.56
  4.5 7.3 %all-to-all-start = ((f32[8,1,8]{2,1,0:T(1,128)}), f32[8,1,8]{2,1,0:T(1,128)S(1)}, u32[]{:S(2)}, u32[]{:S(2)}) async-start(f32[8,1,8]{2,1,0:T(1,128)} %bitcast.5), calls=%async_computation | async-start | bytes 8192 | tf_op jit(solution)/shard_map/all_to_all | solution.py:61
  11.8 0.1 broadcast_in_dim.63
  11.9 0.7 broadcast_compare_fusion
  12.7 4.1 %select_reduce_fusion = f32[32,64]{1,0:T(8,128)S(1)} fusion(f32[32,64,1024]{2,1,0:T(8,128)} %param.3, pred[32,1024]{1,0:T(8,128)(4,1)S(1)} %broadcast_compare_fusion), kind=kLoop, calls=%fused_computation.8 | loop fusion | flops 4192256 | bytes 8429568 | tf_op jit(solution)/shard_map/reduce_sum | solution.py:45
  16.8 0.1 broadcast_divide_fusion.2
  16.9 0.6 gather_fusion.1
  17.5 14.9 %fusion = f32[32,64,64]{2,1,0:T(8,128)S(1)} fusion(f32[32,64,1024]{2,1,0:T(8,128)} %param.3, f32[32,64]{1,0:T(8,128)S(1)} %broadcast_divide_fusion.2, pred[32,1024]{1,0:T(8,128)(4,1)S(1)} %broadcast_compare_fusion), kind=kOutput, calls=%fused_computation.5 | convolution fusion | flops 1614807040 | bytes 8953856 | tf_op jit(solution)/shard_map/svc,swc->svw/dot_general | solution.py:49
  32.4 0.1 bitcast_select_fusion.1
  32.5 0.7 reshape.244
  33.2 0.4 reshape.205
  33.5 0.9 gather_fusion.3
  34.5 6.0 %all-to-all-start.1 = ((f32[8,1,512]{2,1,0:T(1,128)}), f32[8,1,512]{2,1,0:T(1,128)S(1)}, u32[]{:S(2)}, u32[]{:S(2)}) async-start(f32[8,1,512]{2,1,0:T(1,128)} %reshape.244), calls=%async_computation.1 | async-start | bytes 32768 | tf_op jit(solution)/shard_map/all_to_all | solution.py:59
  40.5 0.6 fusion.22
  41.1 6.0 %all-to-all-done.1 = f32[8,1,512]{2,1,0:T(1,128)S(1)} async-done(((f32[8,1,512]{2,1,0:T(1,128)}), f32[8,1,512]{2,1,0:T(1,128)S(1)}, u32[]{:S(2)}, u32[]{:S(2)}) %all-to-all-start.1) | async-done | bytes 16416 | tf_op jit(solution)/shard_map/all_to_all | solution.py:59
  47.1 0.5 broadcast.202
  47.6 0.7 reduce.4
  48.3 0.1 reshape.245
  48.3 0.1 multiply_reduce_fusion
  48.4 0.1 multiply_reduce_fusion.1
  48.5 0.7 reshape.246
  49.2 3.3 %all-to-all-start.2 = ((f32[8,1,512]{2,1,0:T(1,128)}), f32[8,1,512]{2,1,0:T(1,128)S(1)}, u32[]{:S(2)}, u32[]{:S(2)}) async-start(f32[8,1,512]{2,1,0:T(1,128)} %reshape.246), calls=%async_computation.2 | async-start | bytes 32768 | tf_op jit(solution)/shard_map/all_to_all | solution.py:74
  52.6 1.1 bitcast_select_fusion
  53.7 5.4 %all-to-all-done.2 = f32[8,1,512]{2,1,0:T(1,128)S(1)} async-done(((f32[8,1,512]{2,1,0:T(1,128)}), f32[8,1,512]{2,1,0:T(1,128)S(1)}, u32[]{:S(2)}, u32[]{:S(2)}) %all-to-all-start.2) | async-done | bytes 16416 | tf_op jit(solution)/shard_map/all_to_all | solution.py:74
  59.1 3.6 %all-to-all-start.3 = ((f32[8,8,4096]{2,1,0:T(8,128)}), f32[8,8,4096]{2,1,0:T(8,128)S(1)}, u32[]{:S(2)}, u32[]{:S(2)}) async-start(f32[8,8,4096]{2,1,0:T(8,128)} %bitcast_select_fusion), calls=%async_computation.3 | async-start | bytes 2097152 | tf_op jit(solution)/shard_map/all_to_all | solution.py:60
  63.9 0.7 broadcast_multiply_fusion.1
  64.6 41.6 %all-reduce.1 = (f32[64]{0:T(128)S(1)}, f32[]{:T(128)}) all-reduce(f32[64]{0:T(128)S(1)} %get-tuple-element.11, f32[]{:T(128)} %get-tuple-element.5), channel_id=1, replica_groups=mesh['section'=4,'sim'=8] {'section','sim'}, use_global_device_ids=true, to_apply=%region_10.11 | all-reduce | flops 65 | bytes 520 | tf_op jit(solution)/shard_map/psum | solution.py:80
  106.8 1.2 fusion.23
  108.1 0.7 reduce.5
  108.8 0.1 reshape.247
  108.8 1.2 gather_fusion.2
  110.1 0.1 reduce_sum.98
  110.2 0.6 add_reduce_fusion
  110.8 0.1 reshape.206
  110.9 0.7 fusion.6
  111.7 5.3 %all-to-all-start.4 = ((f32[8,8,512]{2,0,1:T(8,128)}), f32[8,8,512]{2,0,1:T(8,128)S(1)}, u32[]{:S(2)}, u32[]{:S(2)}) async-start(f32[8,8,512]{2,0,1:T(8,128)} %fusion.6), calls=%async_computation.4 | async-start | bytes 262144 | tf_op jit(solution)/shard_map/all_to_all | solution.py:73
  117.0 1.0 multiply_add_fusion
  117.9 0.7 div.85
  118.7 40.0 %psum.23 = f32[4096]{0:T(1024)S(1)} all-reduce(f32[4096]{0:T(1024)S(1)} %add.82), channel_id=1, replica_groups=mesh['section'=4,'sim'=8] {'section','sim'}, use_global_device_ids=true, to_apply=%region_12.13 | all-reduce | flops 4096 | bytes 32768 | tf_op jit(solution)/shard_map/psum | solution.py:83
  158.7 0.7 reshape.207
  159.4 0.1 all_to_all.46
  159.6 1.2 gather_fusion.4
  (13 shorter events, 0.2 us)
Async XLA Ops:
  4.5 29.9 %all-to-all-start = ((f32[8,1,8]{2,1,0:T(1,128)}), f32[8,1,8]{2,1,0:T(1,128)S(1)}, u32[]{:S(2)}, u32[]{:S(2)}) async-start(f32[8,1,8]{2,1,0:T(1,128)} %bitcast.5), calls=%async_computation | async-start | bytes 8192 | tf_op jit(solution)/shard_map/all_to_all | solution.py:61
  34.5 12.6 %all-to-all-start.1 = ((f32[8,1,512]{2,1,0:T(1,128)}), f32[8,1,512]{2,1,0:T(1,128)S(1)}, u32[]{:S(2)}, u32[]{:S(2)}) async-start(f32[8,1,512]{2,1,0:T(1,128)} %reshape.244), calls=%async_computation.1 | async-start | bytes 32768 | tf_op jit(solution)/shard_map/all_to_all | solution.py:59
  49.2 9.9 %all-to-all-start.2 = ((f32[8,1,512]{2,1,0:T(1,128)}), f32[8,1,512]{2,1,0:T(1,128)S(1)}, u32[]{:S(2)}, u32[]{:S(2)}) async-start(f32[8,1,512]{2,1,0:T(1,128)} %reshape.246), calls=%async_computation.2 | async-start | bytes 32768 | tf_op jit(solution)/shard_map/all_to_all | solution.py:74
  59.1 51.0 %all-to-all-start.3 = ((f32[8,8,4096]{2,1,0:T(8,128)}), f32[8,8,4096]{2,1,0:T(8,128)S(1)}, u32[]{:S(2)}, u32[]{:S(2)}) async-start(f32[8,8,4096]{2,1,0:T(8,128)} %bitcast_select_fusion), calls=%async_computation.3 | async-start | bytes 2097152 | tf_op jit(solution)/shard_map/all_to_all | solution.py:60
  111.7 47.8 %all-to-all-start.4 = ((f32[8,8,512]{2,0,1:T(8,128)}), f32[8,8,512]{2,0,1:T(8,128)S(1)}, u32[]{:S(2)}, u32[]{:S(2)}) async-start(f32[8,8,512]{2,0,1:T(8,128)} %fusion.6), calls=%async_computation.4 | async-start | bytes 262144 | tf_op jit(solution)/shard_map/all_to_all | solution.py:73
where the time goes:
time: 162 us; the launch traced here: 161 us
  blocking collectives  81.6 us (50%)
  starting transfers between devices  25.5 us (16%)
  matrix products  16.5 us (10%)
  other arithmetic  13.4 us (8%)
  waiting for transfers between devices  11.3 us (7%)
  local copies, waits for them, and re-layouts  9.73 us (6%)
  between operations  2.71 us (2%)
    psum x1, blocking collectives, local(): lax.psum((group_count, group_count * group_mean), ('section', 'sim'))  41.6 us
    psum x1, blocking collectives, local(): lax.psum(group_co + group_count * jnp.outer(gap, gap).reshape(-1), ('sect...  40 us
    dot_general x1, matrix products, local(): jnp.einsum('svc,swc->svw', centered, centered, precision=high)  14.9 us
    all_to_all x1, starting transfers between devices, local(): lax.all_to_all(send_count, 'sim', split_axis=0, concat_axis=0, tiled=True)  7.28 us
    all_to_all x1, starting transfers between devices, local(): lax.all_to_all(send_mean, 'sim', split_axis=0, concat_axis=0, tiled=True)  6.01 us
    all_to_all x1, waiting for transfers between devices, local(): lax.all_to_all(send_mean, 'sim', split_axis=0, concat_axis=0, tiled=True)  5.96 us
    all_to_all x1, waiting for transfers between devices, local(): lax.all_to_all(mean_copies, 'sim', split_axis=1, concat_axis=0, tiled=True)  5.37 us
    all_to_all x1, starting transfers between devices, local(): lax.all_to_all(cov_parts, 'sim', split_axis=1, concat_axis=0, tiled=True)  5.31 us
  transfers between devices with their start and end apart: 5, of which 2 were waited for; matrix products, arithmetic and copies ran while one was open for 19% of the time, Pallas kernels for 0%

commit v1 on v0

--- a/solution.py
+++ b/solution.py
@@ -80,7 +80,9 @@
     total, weighted = lax.psum((group_count, group_count * group_mean), ("section", "sim"))
     global_mean = weighted / total
     gap = group_mean - global_mean
-    spread = lax.psum(group_co + group_count * jnp.outer(gap, gap).reshape(-1), ("section", "sim"))
+    spread = lax.psum(
+        lax.psum(group_co + group_count * jnp.outer(gap, gap).reshape(-1), "section"), "sim"
+    )
     global_cov = (spread / (total - 1.0)).reshape(width, width)
     return (slab_mean, slab_cov, group_cov, global_mean, global_cov)
 

time: 162 us -> 170 us (1.049)
  blocking collectives: 81.6 us -> 89.6 us
    psum x1 -> x2, blocking collectives: 40 us -> 48 us  [the longest x1 37.6 us: local(): lax.psum(lax.psum(group_co + group_count * jnp.outer(gap, gap).reshape(-1...]
  transfers between devices with their start and end apart: 5 -> 5, of which waited for: 2 -> 2; matrix products, arithmetic and copies ran while one was open for 19% -> 18% of each run, Pallas kernels for 0% -> 0%
where the time goes in v1:
time: 170 us; the launch traced here: 169 us
  blocking collectives  89.6 us (53%)
  starting transfers between devices  25.5 us (15%)
  matrix products  16.5 us (10%)
  other arithmetic  13.4 us (8%)
  waiting for transfers between devices  11.3 us (7%)
  local copies, waits for them, and re-layouts  9.73 us (6%)
  between operations  2.71 us (2%)
    psum x1, blocking collectives, local(): lax.psum((group_count, group_count * group_mean), ('section', 'sim'))  41.6 us
    psum x1, blocking collectives, local(): lax.psum(lax.psum(group_co + group_count * jnp.outer(gap, gap).reshape(-1...  37.6 us
    dot_general x1, matrix products, local(): jnp.einsum('svc,swc->svw', centered, centered, precision=high)  14.9 us
    psum x1, blocking collectives, local(): lax.psum(group_co + group_count * jnp.outer(gap, gap).reshape(-1), 'secti...  10.4 us
    all_to_all x1, starting transfers between devices, local(): lax.all_to_all(send_count, 'sim', split_axis=0, concat_axis=0, tiled=True)  7.28 us
    all_to_all x1, starting transfers between devices, local(): lax.all_to_all(send_mean, 'sim', split_axis=0, concat_axis=0, tiled=True)  6.01 us
    all_to_all x1, waiting for transfers between devices, local(): lax.all_to_all(send_mean, 'sim', split_axis=0, concat_axis=0, tiled=True)  5.96 us
    all_to_all x1, waiting for transfers between devices, local(): lax.all_to_all(mean_copies, 'sim', split_axis=1, concat_axis=0, tiled=True)  5.37 us
  transfers between devices with their start and end apart: 5, of which 2 were waited for; matrix products, arithmetic and copies ran while one was open for 18% of the time, Pallas kernels for 0%

profile of v1, /device:TPU:0, one launch (start us, length us, event | category | flops | bytes accessed | tf_op | source)
XLA Modules:
  0.0 168.8 jit_solution(5625787766369307550)
XLA Ops:
  0.6 0.9 convert_reduce_fusion
  1.5 0.7 fusion.19
  2.2 0.1 fusion.10
  2.3 0.1 select_reduce_fusion.1
  2.4 0.7 broadcast_maximum_fusion.1
  3.1 0.8 gather_fusion
  3.9 0.7 select_n.56
  4.5 7.3 %all-to-all-start = ((f32[8,1,8]{2,1,0:T(1,128)}), f32[8,1,8]{2,1,0:T(1,128)S(1)}, u32[]{:S(2)}, u32[]{:S(2)}) async-start(f32[8,1,8]{2,1,0:T(1,128)} %bitcast.5), calls=%async_computation | async-start | bytes 8192 | tf_op jit(solution)/shard_map/all_to_all | solution.py:61
  11.8 0.1 broadcast_in_dim.63
  11.9 0.7 broadcast_compare_fusion
  12.7 4.1 %select_reduce_fusion = f32[32,64]{1,0:T(8,128)S(1)} fusion(f32[32,64,1024]{2,1,0:T(8,128)} %param.3, pred[32,1024]{1,0:T(8,128)(4,1)S(1)} %broadcast_compare_fusion), kind=kLoop, calls=%fused_computation.8 | loop fusion | flops 4192256 | bytes 8429568 | tf_op jit(solution)/shard_map/reduce_sum | solution.py:45
  16.8 0.1 broadcast_divide_fusion.2
  16.9 0.6 gather_fusion.1
  17.5 14.9 %fusion = f32[32,64,64]{2,1,0:T(8,128)S(1)} fusion(f32[32,64,1024]{2,1,0:T(8,128)} %param.3, f32[32,64]{1,0:T(8,128)S(1)} %broadcast_divide_fusion.2, pred[32,1024]{1,0:T(8,128)(4,1)S(1)} %broadcast_compare_fusion), kind=kOutput, calls=%fused_computation.5 | convolution fusion | flops 1614807040 | bytes 8953856 | tf_op jit(solution)/shard_map/svc,swc->svw/dot_general | solution.py:49
  32.4 0.1 bitcast_select_fusion.1
  32.5 0.7 reshape.244
  33.2 0.4 reshape.205
  33.5 0.9 gather_fusion.3
  34.5 6.0 %all-to-all-start.1 = ((f32[8,1,512]{2,1,0:T(1,128)}), f32[8,1,512]{2,1,0:T(1,128)S(1)}, u32[]{:S(2)}, u32[]{:S(2)}) async-start(f32[8,1,512]{2,1,0:T(1,128)} %reshape.244), calls=%async_computation.1 | async-start | bytes 32768 | tf_op jit(solution)/shard_map/all_to_all | solution.py:59
  40.5 0.6 fusion.22
  41.1 6.0 %all-to-all-done.1 = f32[8,1,512]{2,1,0:T(1,128)S(1)} async-done(((f32[8,1,512]{2,1,0:T(1,128)}), f32[8,1,512]{2,1,0:T(1,128)S(1)}, u32[]{:S(2)}, u32[]{:S(2)}) %all-to-all-start.1) | async-done | bytes 16416 | tf_op jit(solution)/shard_map/all_to_all | solution.py:59
  47.1 0.5 broadcast.202
  47.6 0.7 reduce.4
  48.3 0.1 multiply_reduce_fusion
  48.4 0.1 multiply_reduce_fusion.1
  48.5 0.7 reshape.246
  49.2 3.3 %all-to-all-start.2 = ((f32[8,1,512]{2,1,0:T(1,128)}), f32[8,1,512]{2,1,0:T(1,128)S(1)}, u32[]{:S(2)}, u32[]{:S(2)}) async-start(f32[8,1,512]{2,1,0:T(1,128)} %reshape.246), calls=%async_computation.2 | async-start | bytes 32768 | tf_op jit(solution)/shard_map/all_to_all | solution.py:74
  52.6 1.1 bitcast_select_fusion
  53.7 5.4 %all-to-all-done.2 = f32[8,1,512]{2,1,0:T(1,128)S(1)} async-done(((f32[8,1,512]{2,1,0:T(1,128)}), f32[8,1,512]{2,1,0:T(1,128)S(1)}, u32[]{:S(2)}, u32[]{:S(2)}) %all-to-all-start.2) | async-done | bytes 16416 | tf_op jit(solution)/shard_map/all_to_all | solution.py:74
  59.1 3.6 %all-to-all-start.3 = ((f32[8,8,4096]{2,1,0:T(8,128)}), f32[8,8,4096]{2,1,0:T(8,128)S(1)}, u32[]{:S(2)}, u32[]{:S(2)}) async-start(f32[8,8,4096]{2,1,0:T(8,128)} %bitcast_select_fusion), calls=%async_computation.3 | async-start | bytes 2097152 | tf_op jit(solution)/shard_map/all_to_all | solution.py:60
  63.9 0.7 broadcast_multiply_fusion.1
  64.6 41.6 %all-reduce.1 = (f32[64]{0:T(128)S(1)}, f32[]{:T(128)}) all-reduce(f32[64]{0:T(128)S(1)} %get-tuple-element.11, f32[]{:T(128)} %get-tuple-element.5), channel_id=1, replica_groups=mesh['section'=4,'sim'=8] {'section','sim'}, use_global_device_ids=true, to_apply=%region_10.11 | all-reduce | flops 65 | bytes 520 | tf_op jit(solution)/shard_map/psum | solution.py:80
  106.8 1.2 fusion.23
  108.1 0.7 reduce.5
  108.8 0.1 reshape.247
  108.8 1.2 gather_fusion.2
  110.1 0.1 reduce_sum.98
  110.2 0.6 add_reduce_fusion
  110.8 0.1 reshape.206
  110.9 0.7 fusion.6
  111.7 5.3 %all-to-all-start.4 = ((f32[8,8,512]{2,0,1:T(8,128)}), f32[8,8,512]{2,0,1:T(8,128)S(1)}, u32[]{:S(2)}, u32[]{:S(2)}) async-start(f32[8,8,512]{2,0,1:T(8,128)} %fusion.6), calls=%async_computation.4 | async-start | bytes 262144 | tf_op jit(solution)/shard_map/all_to_all | solution.py:73
  117.0 1.0 multiply_add_fusion
  117.9 0.7 div.85
  118.7 10.4 %psum.30 = f32[4096]{0:T(1024)S(1)} all-reduce(f32[4096]{0:T(1024)S(1)} %add.84), channel_id=1, replica_groups=mesh['section'=4,'sim'=8] {'section'}, use_global_device_ids=true, to_apply=%region_12.13 | all-reduce | flops 4096 | bytes 32768 | tf_op jit(solution)/shard_map/psum | solution.py:84
  129.1 37.6 %psum.31 = f32[4096]{0:T(1024)S(1)} all-reduce(f32[4096]{0:T(1024)S(1)} %psum.30), channel_id=1, replica_groups=mesh['section'=4,'sim'=8] {'sim'}, use_global_device_ids=true, to_apply=%region_13.14 | all-reduce | flops 4096 | bytes 32768 | tf_op jit(solution)/shard_map/psum | solution.py:83
  166.7 0.7 reshape.207
  167.4 0.1 all_to_all.46
  167.5 1.2 gather_fusion.4
  (14 shorter events, 0.3 us)
Async XLA Ops:
  4.5 29.9 %all-to-all-start = ((f32[8,1,8]{2,1,0:T(1,128)}), f32[8,1,8]{2,1,0:T(1,128)S(1)}, u32[]{:S(2)}, u32[]{:S(2)}) async-start(f32[8,1,8]{2,1,0:T(1,128)} %bitcast.5), calls=%async_computation | async-start | bytes 8192 | tf_op jit(solution)/shard_map/all_to_all | solution.py:61
  34.5 12.6 %all-to-all-start.1 = ((f32[8,1,512]{2,1,0:T(1,128)}), f32[8,1,512]{2,1,0:T(1,128)S(1)}, u32[]{:S(2)}, u32[]{:S(2)}) async-start(f32[8,1,512]{2,1,0:T(1,128)} %reshape.244), calls=%async_computation.1 | async-start | bytes 32768 | tf_op jit(solution)/shard_map/all_to_all | solution.py:59
  49.2 9.9 %all-to-all-start.2 = ((f32[8,1,512]{2,1,0:T(1,128)}), f32[8,1,512]{2,1,0:T(1,128)S(1)}, u32[]{:S(2)}, u32[]{:S(2)}) async-start(f32[8,1,512]{2,1,0:T(1,128)} %reshape.246), calls=%async_computation.2 | async-start | bytes 32768 | tf_op jit(solution)/shard_map/all_to_all | solution.py:74
  59.1 51.0 %all-to-all-start.3 = ((f32[8,8,4096]{2,1,0:T(8,128)}), f32[8,8,4096]{2,1,0:T(8,128)S(1)}, u32[]{:S(2)}, u32[]{:S(2)}) async-start(f32[8,8,4096]{2,1,0:T(8,128)} %bitcast_select_fusion), calls=%async_computation.3 | async-start | bytes 2097152 | tf_op jit(solution)/shard_map/all_to_all | solution.py:60
  111.7 55.7 %all-to-all-start.4 = ((f32[8,8,512]{2,0,1:T(8,128)}), f32[8,8,512]{2,0,1:T(8,128)S(1)}, u32[]{:S(2)}, u32[]{:S(2)}) async-start(f32[8,8,512]{2,0,1:T(8,128)} %fusion.6), calls=%async_computation.4 | async-start | bytes 262144 | tf_op jit(solution)/shard_map/all_to_all | solution.py:73
